TPU v7x, 256 devices: a whole 4x4x8 slice. The times are simulated.
256 devices in a mesh: seq: 32 (over y, z), head: 8 (over x, core).
Axes of the slice: x: 4, y: 4, z: 8, core: 2. Of those that a mesh axis runs over, the one named last changes fastest.
Arguments:
- tokens: bfloat16 [12288, 4096], P('seq', 'head'), may hold values from -6 to 6
- norm_gain: float32 [4096], replicated, may hold values from 0.25 to 1.75
- w_in: bfloat16 [4096, 8, 2304], P('seq', 'head'), may hold values from -0.09375 to 0.09375
- w_dt: bfloat16 [4096, 128], P('seq', 'head'), may hold values from -0.09375 to 0.09375
- dt_bias: float32 [128], P('head'), may hold values from -3 to -1
- a_log: float32 [128], P('head'), may hold values from -11 to -1
- d_skip: float32 [128], P('head'), may hold values from 0.5 to 1.5
- conv_w: float32 [4, 8, 1280], P(None, 'head'), may hold values from -0.5 to 0.5
- conv_b: float32 [8, 1280], P('head'), may hold values from -0.5 to 0.5
- gate_gain: float32 [8, 1024], P('head'), may hold values from 0.25 to 1.75
- w_out: bfloat16 [8, 1024, 4096], P('head'), may hold values from -0.09375 to 0.09375
Outputs:
- mixed: bfloat16 [12288, 4096], P('seq', 'head')
All inputs are finite; a program needn't handle non-finite values.
Results may differ from a plain program's by a relative error of at most 0.018.
Values may be sent and summed in bfloat16 or wider, within the bound.
A program may use at most 128 MiB of HBM per device.

v0:
```python
from functools import partial
import jax
import jax.numpy as jnp
from jax import lax
from jax.sharding import Mesh
from jax.sharding import PartitionSpec as P

STRETCH = 128
SEQ = ("seq_0", "seq_1")
EPS = 1e-05
HIGHEST = lax.Precision.HIGHEST


def from_behind(shard, axis, by):
    count = lax.axis_size(axis)
    pairs = [(i, i + by) for i in range(count) if 0 <= i + by < count]
    return lax.ppermute(shard, axis, pairs)


def sent_together(arrays, axis, dim, along):
    both = jnp.concatenate(arrays, axis=along)
    result, at, gathered = (lax.all_gather(both, axis, axis=dim, tiled=True), 0, [])
    for a in arrays:
        gathered.append(lax.slice_in_dim(result, at, at + a.shape[along], axis=along))
        at += a.shape[along]
    return tuple(gathered)


def neutral_like(shard, identity):
    return jax.tree.map(
        lambda part, zero: jnp.zeros_like(part) + jnp.asarray(zero, part.dtype), shard, identity
    )


def entering(shard, axes, combine, identity):
    before = start = neutral_like(shard, identity)
    running = shard
    for axis in reversed(axes):
        count, index = (lax.axis_size(axis), lax.axis_index(axis))
        pieces = jax.tree.map(
            lambda part, kind: lax.all_gather(part.astype(kind), axis),
            running,
            (jnp.bfloat16, jnp.bfloat16),
        )
        inside, running = (start, start)
        for k in range(count):
            passed = k < index
            running = combine(
                running, jax.tree.map(lambda part, own: part[k].astype(own.dtype), pieces, shard)
            )
            inside = jax.tree.map(lambda new, old: jnp.where(passed, new, old), running, inside)
        before = combine(inside, before)
    return before


def normalize(values, gain):
    squares = jnp.mean(values * values, axis=-1, keepdims=True)
    return values * lax.rsqrt(squares + EPS) * gain


def state_block(inputs, step_size, log_decay, in_map, out_map, block_len):
    length = inputs.shape[0]
    stretch_count = length // block_len
    head_count = inputs.shape[1]
    head_size = inputs.shape[2]
    state_size = in_map.shape[1]
    shaped = (
        inputs.reshape(stretch_count, block_len, head_count, head_size),
        step_size.reshape(stretch_count, block_len, head_count),
        log_decay.reshape(stretch_count, block_len, head_count),
        in_map.reshape(stretch_count, block_len, state_size),
        out_map.reshape(stretch_count, block_len, state_size),
    )
    causal = jnp.arange(block_len)[:, None] >= jnp.arange(block_len)[None, :]

    def advance(state_now, pieces):
        stretch_in, stretch_step, stretch_log, stretch_b, stretch_c = pieces
        cumulative = jnp.cumsum(stretch_log, axis=0)
        gap_log = cumulative[:, None, :] - cumulative[None, :, :]
        decays = jnp.where(
            causal[:, :, None], jnp.exp(jnp.where(causal[:, :, None], gap_log, 0.0)), 0.0
        )
        scores = jnp.dot(stretch_c, stretch_b.T, preferred_element_type=jnp.float32)
        wide_c = stretch_c.astype(jnp.float32)
        wide_b = stretch_b.astype(jnp.float32)
        weights = scores[:, :, None] * decays * stretch_step[None, :, :]
        within = jnp.einsum("ijh,jhp->ihp", weights, stretch_in, precision=HIGHEST)
        across = jnp.exp(cumulative)[:, :, None] * jnp.einsum(
            "in,hpn->ihp", wide_c, state_now, precision=HIGHEST
        )
        to_end = jnp.exp(cumulative[-1][None, :] - cumulative) * stretch_step
        fresh_state = jnp.einsum("jh,jhp,jn->hpn", to_end, stretch_in, wide_b, precision=HIGHEST)
        state_next = jnp.exp(cumulative[-1])[:, None, None] * state_now + fresh_state
        return (state_next, within + across)

    start_state = jnp.zeros((head_count, head_size, state_size), jnp.float32)
    final, outputs = lax.scan(advance, start_state, shaped)
    return (outputs.reshape(length, head_count, head_size), final)


def link_states(earlier, later):
    return (earlier[0] + later[0], jnp.exp(later[0])[:, :, None, None] * earlier[1] + later[1])


def body(tokens, norm_gain, w_in, w_dt, dt_bias, a_log, d_skip, conv_w, conv_b, gate_gain, w_out):
    local_rows = tokens.shape[0]
    kernel_len = conv_w.shape[0]
    groups, group_width = gate_gain.shape
    head_count = dt_bias.shape[0]
    per_group = head_count // groups
    head_size = group_width // per_group
    state_size = (conv_b.shape[1] - group_width) // 2
    gathered = lax.all_gather(tokens, "head", axis=1, tiled=True)
    normed = normalize(gathered.astype(jnp.float32), norm_gain).astype(jnp.bfloat16)
    before = from_behind(normed[local_rows - kernel_len + 1 :], SEQ, 1)
    source = jnp.concatenate([before, normed], axis=0)
    span_rows = source.shape[0]
    flat_in = w_in.reshape(w_in.shape[0], groups * w_in.shape[2])
    pieces = sent_together((flat_in, w_dt), SEQ, 0, 1)
    proj_sum = jnp.dot(source, pieces[0], preferred_element_type=jnp.float32)
    step_sum = jnp.dot(source, pieces[1], preferred_element_type=jnp.float32)
    projected = proj_sum.astype(jnp.bfloat16).reshape(span_rows, groups, w_in.shape[2])
    step_size = jax.nn.softplus(step_sum[span_rows - local_rows :] + dt_bias[None, :])
    gate_raw = projected[span_rows - local_rows :, :, :group_width]
    extended = projected[:, :, group_width:]
    summed = conv_b[None, :, :]
    for offset in range(kernel_len):
        summed = summed + conv_w[offset][None, :, :] * extended[
            offset : offset + local_rows
        ].astype(jnp.float32)
    narrow = lax.optimization_barrier(jax.nn.silu(summed).astype(jnp.bfloat16))
    convolved = narrow.astype(jnp.float32)
    inputs = convolved[:, :, :group_width].reshape(local_rows, groups, per_group, head_size)
    in_map = narrow[:, :, group_width : group_width + state_size]
    out_map = narrow[:, :, group_width + state_size :]
    step_grouped = step_size.reshape(local_rows, groups, per_group)
    log_decay = -jnp.exp(a_log).reshape(groups, per_group)[None, :, :] * step_grouped
    run_block = jax.vmap(
        partial(state_block, block_len=STRETCH), in_axes=(1, 1, 1, 1, 1), out_axes=(1, 0)
    )
    local_out, ending = run_block(inputs, step_grouped, log_decay, in_map, out_map)
    totals = jnp.sum(log_decay, axis=0)
    identity = (jnp.zeros_like(totals), jnp.zeros_like(ending))
    prior_decay, incoming = entering((totals, ending), SEQ, link_states, identity)
    cumulative = jnp.exp(jnp.cumsum(log_decay, axis=0))
    carried = (
        jnp.einsum("tgn,ghpn->tghp", out_map.astype(jnp.float32), incoming, precision=HIGHEST)
        * cumulative[:, :, :, None]
    )
    outputs = local_out + carried + d_skip.reshape(groups, per_group)[None, :, :, None] * inputs
    gated = outputs.reshape(local_rows, groups, group_width) * jax.nn.silu(
        gate_raw.astype(jnp.float32)
    )
    normed_out = normalize(gated, gate_gain[None, :, :]).astype(jnp.bfloat16)
    flat_out = normed_out.reshape(local_rows, groups * group_width)
    terms = jnp.dot(
        flat_out,
        w_out.reshape(groups * group_width, w_out.shape[2]),
        preferred_element_type=jnp.float32,
    )
    return lax.psum_scatter(terms.astype(jnp.bfloat16), "head", scatter_dimension=1, tiled=True)


def solution(mesh):
    split = Mesh(mesh.devices.reshape(4, 8, mesh.shape["head"]), ("seq_0", "seq_1", "head"))
    in_specs = (
        P(SEQ, "head"),
        P(),
        P(SEQ, "head", None),
        P(SEQ, "head"),
        P("head"),
        P("head"),
        P("head"),
        P(None, "head", None),
        P("head", None),
        P("head", None),
        P("head", None, None),
    )
    out_specs = P(SEQ, "head")
    return jax.shard_map(body, mesh=split, in_specs=in_specs, out_specs=out_specs, check_vma=False)
```

profile of v0, /device:TPU:8, one launch (start us, length us, event | category | flops | bytes accessed | tf_op | source)
XLA Modules:
  0.0 413.0 jit_solution(1749421173129096668)
XLA Ops:
  10.2 32.1 %all-gather.7.cloned.1.call-done = bf16[384,4096]{1,0:T(8,128)(2,1)} async-done(((bf16[384,512]{1,0:T(8,128)(2,1)}), bf16[384,4096]{1,0:T(8,128)(2,1)}) %all-gather.7.cloned.1.call-update) | async-done | bytes 3145744 | tf_op jit(solution)/shard_map/all_gather | solution.py:113
  42.3 2.7 fusion.45
  46.3 3.5 collective-permute-start
  49.9 4.3 %collective-permute-done = bf16[3,4096]{1,0:T(4,128)(2,1)S(1)} collective-permute-done((bf16[3,4096]{1,0:T(4,128)(2,1)S(1)}, bf16[3,4096]{1,0:T(4,128)(2,1)S(1)}, u32[]{:S(2)}, u32[]{:S(2)}) %collective-permute-start) | collective-permute-done | bytes 24608 | tf_op jit(solution)/shard_map/ppermute | solution.py:17
  54.2 145.0 %all-gather.9.cloned.1.call-done = bf16[4096,2320]{1,0:T(8,128)(2,1)} async-done(((bf16[128,2320]{1,0:T(8,128)(2,1)}), bf16[4096,2320]{1,0:T(8,128)(2,1)}) %all-gather.9.cloned.1.call-update) | async-done | bytes 19005456 | tf_op jit(solution)/shard_map/all_gather | solution.py:22
  199.2 13.4 %fusion.54 = bf16[387,1,2304]{2,0,1:T(8,128)(2,1)S(1)} fusion(bf16[4096,2320]{1,0:T(8,128)(2,1)} %all-gather.9.cloned.1.call-done, bf16[384,4096]{1,0:T(8,128)(2,1)} %copy-done.4, bf16[3,4096]{1,0:T(4,128)(2,1)S(1)} %collective-permute-done), kind=kOutput, calls=%fused_computation.61 | convolution fusion | flops 7311612928 | bytes 23827968 | tf_op jit(solution)/shard_map/dot_general | solution.py:120
  215.5 2.3 fusion.162
  220.2 3.2 copy.55
  223.4 59.6 %while.14 = (s32[]{:T(128)}, f32[1,16,64,128]{3,2,1,0:T(8,128)S(1)}, f32[3,1,128,16,64]{2,0,4,3,1:T(4,128)}, f32[3,1,128,16]{3,2,1,0:T(8,128)S(1)}, f32[3,1,128,...) while((s32[]{:T(128)}, ...), condition=%wide.region_3.4_spmd.clone.clone, body=%wide.region_1.3_spmd.clone.clone.sunk | while | flops 610682880 | bytes 5721559 | solution.py:97
  224.5 3.3 fusion.191
  229.4 13.8 %dynamic_update_slice.7 = f32[3,1,128,16,64]{2,0,4,3,1:T(4,128)} dynamic-update-slice(f32[3,1,128,16,64]{2,0,4,3,1:T(4,128)} %get-tuple-element.246, f32[1,1,128,16,64]{2,0,4,3,1:T(1,128)S(1)} %bitcast.242, s32[]{:T(128)S(6)} %copy.92, s32[]{:T(128)} %constant.25.clone.1..sunk, s32[]{:T(128)} %constant.25.clone.1..sunk, s32[]{:T(128)} %constant.25.clone.1..sunk, s32[]{:T(128)} %constant.25.clone.1..sunk) | dynamic-update-slice | bytes 1048580 | tf_op jit(solution)/shard_map/vmap()/while/body/jit(dynamic_update_index_in_dim)/dynamic_update_slice | solution.py:97
  244.4 3.3 fusion.191
  249.3 13.8 %dynamic_update_slice.7 = f32[3,1,128,16,64]{2,0,4,3,1:T(4,128)} dynamic-update-slice(f32[3,1,128,16,64]{2,0,4,3,1:T(4,128)} %get-tuple-element.246, f32[1,1,128,16,64]{2,0,4,3,1:T(1,128)S(1)} %bitcast.242, s32[]{:T(128)S(6)} %copy.92, s32[]{:T(128)} %constant.25.clone.1..sunk, s32[]{:T(128)} %constant.25.clone.1..sunk, s32[]{:T(128)} %constant.25.clone.1..sunk, s32[]{:T(128)} %constant.25.clone.1..sunk) | dynamic-update-slice | bytes 1048580 | tf_op jit(solution)/shard_map/vmap()/while/body/jit(dynamic_update_index_in_dim)/dynamic_update_slice | solution.py:97
  264.3 3.3 fusion.191
  269.2 13.8 %dynamic_update_slice.7 = f32[3,1,128,16,64]{2,0,4,3,1:T(4,128)} dynamic-update-slice(f32[3,1,128,16,64]{2,0,4,3,1:T(4,128)} %get-tuple-element.246, f32[1,1,128,16,64]{2,0,4,3,1:T(1,128)S(1)} %bitcast.242, s32[]{:T(128)S(6)} %copy.92, s32[]{:T(128)} %constant.25.clone.1..sunk, s32[]{:T(128)} %constant.25.clone.1..sunk, s32[]{:T(128)} %constant.25.clone.1..sunk, s32[]{:T(128)} %constant.25.clone.1..sunk) | dynamic-update-slice | bytes 1048580 | tf_op jit(solution)/shard_map/vmap()/while/body/jit(dynamic_update_index_in_dim)/dynamic_update_slice | solution.py:97
  285.4 15.7 %all-reduce = bf16[128]{0:T(256)(128)(2,1)S(1)} all-reduce(bf16[128]{0:T(256)(128)(2,1)S(1)} %dynamic-update-slice), channel_id=2, replica_groups=mesh['seq_0'=4,'seq_1'=8,'head'=8] {'seq_1'}, use_global_device_ids=true, to_apply=%add | all-reduce | flops 128 | bytes 512
  301.3 21.9 %all-gather.13.cloned.1.call-done = bf16[8,16,64,128]{3,2,1,0:T(8,128)(2,1)} async-done(((bf16[1,16,64,128]{3,2,1,0:T(8,128)(2,1)}), bf16[8,16,64,128]{3,2,1,0:T(8,128)(2,1)}) %all-gather.13.cloned.1.call-update) | async-done | bytes 2097168 | tf_op jit(solution)/shard_map/all_gather | solution.py:41
  323.1 2.8 fusion.106
  326.0 8.1 %all_gather.27 = bf16[4,1,16]{2,1,0:T(2,128)(2,1)S(1)} all-gather(bf16[1,1,16]{2,1,0:T(2,128)(2,1)S(1)} %get-tuple-element.156), channel_id=1, replica_groups=mesh['seq_0'=4,'seq_1'=8,'head'=8] {'seq_0'}, dimensions={0}, use_global_device_ids=true | all-gather | bytes 160 | tf_op jit(solution)/shard_map/all_gather | solution.py:41
  335.8 2.8 transpose.64
  338.7 11.5 %all-gather.11.cloned.1.call-done = bf16[4,1,16,64,128]{4,3,2,1,0:T(8,128)(2,1)} async-done(((bf16[1,1,16,64,128]{4,3,2,1,0:T(8,128)(2,1)}), bf16[4,1,16,64,128]{4,3,2,1,0:T(8,128)(2,1)}) %all-gather.11.cloned.1.call-update) | async-done | bytes 1048592 | tf_op jit(solution)/shard_map/all_gather | solution.py:41
  350.2 4.7 %fusion.69 = f32[384,1,16,64]{0,3,2,1:T(8,128)} fusion(f32[384,1,16,64]{0,3,2,1:T(8,128)S(1)} %transpose.64, f32[384,1,16,64]{0,3,2,1:T(8,128)S(1)} %bitcast.245, f32[16]{0:T(128)S(1)} %copy-done.12, f32[384,16]{0,1:T(8,128)S(1)} %fusion.139, bf16[4,1,16,64,128]{4,3,2,1,0:T(8,128)(2,1)} %all-gather.11.cloned.1.call-done, f32[16]{0:T(128)S(1)} %get-tuple-element.173, ...), kind=kOutput, calls=%fused_computation.78 | convolution fusion | flops 611844096 | bytes 7988108 | tf_op jit(solution)/shard_map/tgn,ghpn->tghp/dot_general | solution.py:147
  357.6 8.7 %fusion.48 = bf16[384,4096]{1,0:T(8,128)(2,1)} fusion(bf16[1,1024,4096]{2,1,0:T(8,128)(2,1)} %param.23, f32[1024]{0:T(1024)S(1)} %bitcast.251, f32[384]{0:T(512)S(1)} %add_rsqrt_fusion, f32[384,1,1024]{2,0,1:T(8,128)S(1)} %copy.63, bf16[387,1,2304]{2,0,1:T(8,128)(2,1)S(1)} %copy-done.2), kind=kOutput, calls=%fused_computation.59 | convolution fusion | flops 3226337280 | bytes 13899776 | tf_op jit(solution)/shard_map/dot_general | solution.py:156
  366.4 40.1 %reduce-scatter.2.cloned.1.call-done = bf16[384,512]{1,0:T(8,128)(2,1)} async-done(((bf16[384,4096]{1,0:T(8,128)(2,1)}), bf16[384,512]{1,0:T(8,128)(2,1)}) %reduce-scatter.2.cloned.1.call-update) | async-done | bytes 393232 | tf_op jit(solution)/shard_map/reduce_scatter | solution.py:161
  (114 shorter events, 24.6 us)
Async XLA Ops:
  6.5 3.6 copy-start.10
  6.5 35.8 %all-gather.7.cloned.1.call-start = ((), (), s32[]{:S(2)}) async-start(), calls=%async_computation.1 | async-start | bytes 3538944 | tf_op jit(solution)/shard_map/all_gather | solution.py:113
  7.3 191.9 %all-gather.9.cloned.1.call-start = ((), (), s32[]{:S(2)}) async-start(), calls=%async_computation.2 | async-start | bytes 20545536 | tf_op jit(solution)/shard_map/all_gather | solution.py:22
  10.1 34.9 %copy-start.7 = (f32[4096]{0:T(1024)S(1)}, f32[4096]{0:T(1024)}, u32[]{:S(2)}) copy-start(f32[4096]{0:T(1024)} %param.14) | copy-start | bytes 49156
  10.1 313.0 %all-gather.13.cloned.1.call-start = ((), (), s32[]{:S(2)}) async-start(), calls=%async_computation.5 | async-start | bytes 2359296 | tf_op jit(solution)/shard_map/all_gather | solution.py:41
  42.3 2.8 copy-start
  45.1 4.6 %copy-start.6 = (f32[4,1,1280]{2,1,0:T(1,128)S(1)}, f32[4,1,1280]{2,1,0:T(1,128)}, u32[]{:S(2)}) copy-start(f32[4,1,1280]{2,1,0:T(1,128)} %param.20) | copy-start | bytes 61444
  45.1 4.7 %copy-start.8 = (f32[1,1280]{1,0:T(1,128)S(1)}, f32[1,1280]{1,0:T(1,128)}, u32[]{:S(2)}) copy-start(f32[1,1280]{1,0:T(1,128)} %param.21) | copy-start | bytes 15364
  46.2 3.5 copy-start.4
  46.3 7.9 %collective-permute-start = (bf16[3,4096]{1,0:T(4,128)(2,1)S(1)}, bf16[3,4096]{1,0:T(4,128)(2,1)S(1)}, u32[]{:S(2)}, u32[]{:S(2)}) collective-permute-start(bf16[3,4096]{1,0:T(4,128)(2,1)S(1)} %slice.201), channel_id=1, source_target_pairs={{0,8},{8,16},{16,24},{24,32},{32,40},{40,48},{48,56},{56,64},{64,7... | collective-permute-start | bytes 73736 | tf_op jit(solution)/shard_map/ppermute | solution.py:17
  212.6 1.3 copy-start.1
  212.6 2.9 copy-start.5
  213.9 3.9 copy-start.3
  213.9 1.5 copy-start.11
  223.4 60.5 %copy-start.13 = (u32[256]{0:T(256)S(1)}, u32[256]{0:T(256)}, u32[]{:S(2)}) copy-start(u32[256]{0:T(256)} %constant.77) | copy-start | bytes 3076
  283.8 66.4 %all-gather.11.cloned.1.call-start = ((), (), s32[]{:S(2)}) async-start(), calls=%async_computation.3 | async-start | bytes 1310720 | tf_op jit(solution)/shard_map/all_gather | solution.py:41
  325.9 80.6 %reduce-scatter.2.cloned.1.call-start = ((), (), s32[]{:S(2)}) async-start(), calls=%async_computation.4 | async-start | bytes 3538944 | tf_op jit(solution)/shard_map/reduce_scatter | solution.py:161
  335.4 14.7 %copy-start.12 = (f32[16]{0:T(128)S(1)}, f32[16]{0:T(128)}, u32[]{:S(2)}) copy-start(f32[16]{0:T(128)} %param.19) | copy-start | bytes 196
  354.9 2.0 copy-start.2
  356.9 0.7 copy-start.9
Sparse Core Ops, SparseCore 0:
  9.2 33.0 all-gather.6
  44.9 154.2 all-gather.8
  283.9 39.1 all-gather.12
  326.1 24.0 all-gather.10
  366.5 39.9 reduce-scatter.1
where the time goes:
time: 415 us; the launch traced here: 413 us
  waiting for transfers between devices  256 us (62%)
  local copies, waits for them, and re-layouts  56.8 us (14%)
  matrix products  45.5 us (11%)
  blocking collectives  23.8 us (6%)
  between operations  14.1 us (3%)
  other arithmetic  13.3 us (3%)
    all_gather x1, waiting for transfers between devices, sent_together(): lax.all_gather(both, axis, axis=dim, tiled=True)  145 us
    dynamic_update_slice x3, local copies, waits for them, and re-layouts, state_block(): final, outputs = lax.scan(advance, start_state, shaped)  41.5 us
    reduce_scatter x1, waiting for transfers between devices, body(): lax.psum_scatter(terms.astype(jnp.bfloat16), 'head', scatter_dimension=1,...  40.1 us
    all_gather x2, waiting for transfers between devices, entering(): lax.all_gather(part.astype(kind), axis)  33.4 us
    all_gather x1, waiting for transfers between devices, body(): gathered = lax.all_gather(tokens, 'head', axis=1, tiled=True)  32.1 us
    unnamed x1, blocking collectives  15.7 us
    dot_general x1, matrix products, body(): proj_sum = jnp.dot(source, pieces[0], preferred_element_type=jnp.float32)  13.4 us
    dot_general x3, matrix products, advance(): within = jnp.einsum('ijh,jhp->ihp', weights, stretch_in, precision=HIGHEST)  9.81 us
  transfers between devices with their start and end apart: 6, of which 6 were waited for; matrix products, arithmetic and copies ran while one was open for 3% of the time, Pallas kernels for 0%

commit v1 on v0

--- a/solution.py
+++ b/solution.py
@@ -110,7 +110,9 @@
     per_group = head_count // groups
     head_size = group_width // per_group
     state_size = (conv_b.shape[1] - group_width) // 2
-    gathered = lax.all_gather(tokens, "head", axis=1, tiled=True)
+    now = lax.axis_size("head")
+    raw_out = jnp.concatenate([tokens] * now, axis=1)
+    gathered = lax.all_to_all(raw_out, split_axis=1, tiled=True, concat_axis=1, axis_name="head")
     normed = normalize(gathered.astype(jnp.float32), norm_gain).astype(jnp.bfloat16)
     before = from_behind(normed[local_rows - kernel_len + 1 :], SEQ, 1)
     source = jnp.concatenate([before, normed], axis=0)

time: 415 us -> 390 us (0.940)
  waiting for transfers between devices: 256 us -> 209 us
  local copies, waits for them, and re-layouts: 56.8 us -> 70.5 us
  starting transfers between devices: 3.63 us -> 8.92 us
    all_gather x1, waiting for transfers between devices: 145 us -> 91.9 us  [sent_together(): lax.all_gather(both, axis, axis=dim, tiled=True)]
    all_to_all x0 -> x1, waiting for transfers between devices: none -> 38.3 us  [body(): lax.all_to_all(raw_out, split_axis=1, tiled=True, concat_axis=1, axis_nam...]
    all_gather x1 -> x0, waiting for transfers between devices: 32.1 us -> none  [body(): gathered = lax.all_gather(tokens, 'head', axis=1, tiled=True)]
    all_to_all x0 -> x2, local copies, waits for them, and re-layouts: none -> 6.41 us  [body(): lax.all_to_all(raw_out, split_axis=1, tiled=True, concat_axis=1, axis_nam...]
    all_to_all x0 -> x1, starting transfers between devices: none -> 4.57 us  [body(): lax.all_to_all(raw_out, split_axis=1, tiled=True, concat_axis=1, axis_nam...]
  transfers between devices with their start and end apart: 6 -> 6, of which waited for: 6 -> 6; matrix products, arithmetic and copies ran while one was open for 3% -> 5% of each run, Pallas kernels for 0% -> 0%
where the time goes in v1:
time: 390 us; the launch traced here: 388 us
  waiting for transfers between devices  209 us (54%)
  local copies, waits for them, and re-layouts  70.5 us (18%)
  matrix products  47.3 us (12%)
  blocking collectives  23.5 us (6%)
  other arithmetic  14.8 us (4%)
  between operations  14.1 us (4%)
  starting transfers between devices  8.92 us (2%)
    all_gather x1, waiting for transfers between devices, sent_together(): lax.all_gather(both, axis, axis=dim, tiled=True)  91.9 us
    dynamic_update_slice x3, local copies, waits for them, and re-layouts, state_block(): final, outputs = lax.scan(advance, start_state, shaped)  41.5 us
    reduce_scatter x1, waiting for transfers between devices, body(): lax.psum_scatter(terms.astype(jnp.bfloat16), 'head', scatter_dimension=1,...  40.1 us
    all_to_all x1, waiting for transfers between devices, body(): lax.all_to_all(raw_out, split_axis=1, tiled=True, concat_axis=1, axis_nam...  38.3 us
    all_gather x2, waiting for transfers between devices, entering(): lax.all_gather(part.astype(kind), axis)  32.1 us
    unnamed x1, blocking collectives  15.7 us
    dot_general x1, matrix products, body(): proj_sum = jnp.dot(source, pieces[0], preferred_element_type=jnp.float32)  14.2 us
    dot_general x3, matrix products, advance(): within = jnp.einsum('ijh,jhp->ihp', weights, stretch_in, precision=HIGHEST)  9.8 us
  transfers between devices with their start and end apart: 6, of which 6 were waited for; matrix products, arithmetic and copies ran while one was open for 5% of the time, Pallas kernels for 0%

profile of v1, /device:TPU:8, one launch (start us, length us, event | category | flops | bytes accessed | tf_op | source)
XLA Modules:
  0.0 387.9 jit_solution(8331059611487835285)
XLA Ops:
  10.1 3.0 copy.105
  13.1 4.6 %all-to-all-start = ((bf16[384,8,512]{2,0,1:T(8,128)(2,1)}), bf16[384,8,512]{2,0,1:T(8,128)(2,1)}, u32[]{:S(2)}, u32[]{:S(2)}) async-start(bf16[384,8,512]{2,0,1:T(8,128)(2,1)} %copy.105), calls=%async_computation | async-start | bytes 6291456 | tf_op jit(solution)/shard_map/all_to_all | solution.py:115
  17.7 38.3 %all-to-all-done = bf16[384,8,512]{2,0,1:T(8,128)(2,1)} async-done(((bf16[384,8,512]{2,0,1:T(8,128)(2,1)}), bf16[384,8,512]{2,0,1:T(8,128)(2,1)}, u32[]{:S(2)}, u32[]{:S(2)}) %all-to-all-start) | async-done | bytes 3145760 | tf_op jit(solution)/shard_map/all_to_all | solution.py:115
  56.1 3.5 copy.106
  64.4 4.0 %collective-permute-start = (bf16[3,4096]{1,0:T(4,128)(2,1)S(1)}, bf16[3,4096]{1,0:T(4,128)(2,1)S(1)}, u32[]{:S(2)}, u32[]{:S(2)}) collective-permute-start(bf16[3,4096]{1,0:T(4,128)(2,1)S(1)} %copy.107), channel_id=1, source_target_pairs={{0,8},{8,16},{16,24},{24,32},{32,40},{40,48},{48,56},{56,64},{64,7... | collective-permute-start | bytes 73736 | tf_op jit(solution)/shard_map/ppermute | solution.py:17
  68.6 6.1 %collective-permute-done = bf16[3,4096]{1,0:T(4,128)(2,1)S(1)} collective-permute-done((bf16[3,4096]{1,0:T(4,128)(2,1)S(1)}, bf16[3,4096]{1,0:T(4,128)(2,1)S(1)}, u32[]{:S(2)}, u32[]{:S(2)}) %collective-permute-start) | collective-permute-done | bytes 24608 | tf_op jit(solution)/shard_map/ppermute | solution.py:17
  75.2 91.9 %all-gather.6.cloned.1.call-done = bf16[4096,2320]{1,0:T(8,128)(2,1)} async-done(((bf16[128,2320]{1,0:T(8,128)(2,1)}), bf16[4096,2320]{1,0:T(8,128)(2,1)}) %all-gather.6.cloned.1.call-update) | async-done | bytes 19005456 | tf_op jit(solution)/shard_map/all_gather | solution.py:22
  167.1 14.2 %fusion.56 = bf16[387,1,2304]{2,0,1:T(8,128)(2,1)S(1)} fusion(bf16[4096,2320]{1,0:T(8,128)(2,1)} %all-gather.6.cloned.1.call-done, bf16[384,4096]{0,1:T(8,128)(2,1)} %fusion.46, bf16[3,4096]{0,1:T(8,128)(2,1)S(1)} %copy.108), kind=kOutput, calls=%fused_computation.63 | convolution fusion | flops 7311612928 | bytes 23827968 | tf_op jit(solution)/shard_map/dot_general | solution.py:122
  183.4 3.1 fusion.163
  190.2 3.2 copy.113
  193.4 64.6 %while.14 = (s32[]{:T(128)}, f32[1,16,64,128]{3,2,1,0:T(8,128)S(1)}, f32[3,1,128,16,64]{2,0,4,3,1:T(4,128)}, f32[3,1,128,16]{3,2,1,0:T(8,128)}, f32[3,1,128,16]{...) while((s32[]{:T(128)}, ...), condition=%wide.region_3.4_spmd.clone.clone, body=%wide.region_1.3_spmd.clone.clone.sunk | while | flops 610682880 | bytes 5721559 | solution.py:97
  197.9 3.3 fusion.192
  201.1 13.8 %dynamic_update_slice.7 = f32[3,1,128,16,64]{2,0,4,3,1:T(4,128)} dynamic-update-slice(f32[3,1,128,16,64]{2,0,4,3,1:T(4,128)} %get-tuple-element.262, f32[1,1,128,16,64]{2,0,4,3,1:T(1,128)S(1)} %bitcast.249, s32[]{:T(128)S(6)} %copy.157, s32[]{:T(128)} %constant.25.clone.1..sunk, s32[]{:T(128)} %constant.25.clone.1..sunk, s32[]{:T(128)} %constant.25.clone.1..sunk, s32[]{:T(128)} %constant.25.clone.1..sunk) | dynamic-update-slice | bytes 1048580 | tf_op jit(solution)/shard_map/vmap()/while/body/jit(dynamic_update_index_in_dim)/dynamic_update_slice | solution.py:97
  219.4 3.3 fusion.192
  222.7 13.8 %dynamic_update_slice.7 = f32[3,1,128,16,64]{2,0,4,3,1:T(4,128)} dynamic-update-slice(f32[3,1,128,16,64]{2,0,4,3,1:T(4,128)} %get-tuple-element.262, f32[1,1,128,16,64]{2,0,4,3,1:T(1,128)S(1)} %bitcast.249, s32[]{:T(128)S(6)} %copy.157, s32[]{:T(128)} %constant.25.clone.1..sunk, s32[]{:T(128)} %constant.25.clone.1..sunk, s32[]{:T(128)} %constant.25.clone.1..sunk, s32[]{:T(128)} %constant.25.clone.1..sunk) | dynamic-update-slice | bytes 1048580 | tf_op jit(solution)/shard_map/vmap()/while/body/jit(dynamic_update_index_in_dim)/dynamic_update_slice | solution.py:97
  240.9 3.3 fusion.192
  244.2 13.8 %dynamic_update_slice.7 = f32[3,1,128,16,64]{2,0,4,3,1:T(4,128)} dynamic-update-slice(f32[3,1,128,16,64]{2,0,4,3,1:T(4,128)} %get-tuple-element.262, f32[1,1,128,16,64]{2,0,4,3,1:T(1,128)S(1)} %bitcast.249, s32[]{:T(128)S(6)} %copy.157, s32[]{:T(128)} %constant.25.clone.1..sunk, s32[]{:T(128)} %constant.25.clone.1..sunk, s32[]{:T(128)} %constant.25.clone.1..sunk, s32[]{:T(128)} %constant.25.clone.1..sunk) | dynamic-update-slice | bytes 1048580 | tf_op jit(solution)/shard_map/vmap()/while/body/jit(dynamic_update_index_in_dim)/dynamic_update_slice | solution.py:97
  260.6 15.7 %all-reduce = bf16[128]{0:T(256)(128)(2,1)S(1)} all-reduce(bf16[128]{0:T(256)(128)(2,1)S(1)} %dynamic-update-slice), channel_id=2, replica_groups=mesh['seq_0'=4,'seq_1'=8,'head'=8] {'seq_1'}, use_global_device_ids=true, to_apply=%add | all-reduce | flops 128 | bytes 512
  276.4 21.7 %all-gather.10.cloned.1.call-done = bf16[8,16,64,128]{3,2,1,0:T(8,128)(2,1)} async-done(((bf16[1,16,64,128]{3,2,1,0:T(8,128)(2,1)}), bf16[8,16,64,128]{3,2,1,0:T(8,128)(2,1)}) %all-gather.10.cloned.1.call-update) | async-done | bytes 2097168 | tf_op jit(solution)/shard_map/all_gather | solution.py:41
  301.0 7.8 %all_gather.23 = bf16[4,1,16]{2,1,0:T(2,128)(2,1)S(1)} all-gather(bf16[1,1,16]{2,1,0:T(2,128)(2,1)S(1)} %get-tuple-element.172), channel_id=1, replica_groups=mesh['seq_0'=4,'seq_1'=8,'head'=8] {'seq_0'}, dimensions={0}, use_global_device_ids=true | all-gather | bytes 160 | tf_op jit(solution)/shard_map/all_gather | solution.py:41
  314.7 10.3 %all-gather.8.cloned.1.call-done = bf16[4,1,16,64,128]{4,3,2,1,0:T(8,128)(2,1)} async-done(((bf16[1,1,16,64,128]{4,3,2,1,0:T(8,128)(2,1)}), bf16[4,1,16,64,128]{4,3,2,1,0:T(8,128)(2,1)}) %all-gather.8.cloned.1.call-update) | async-done | bytes 1048592 | tf_op jit(solution)/shard_map/all_gather | solution.py:41
  325.0 4.7 %fusion.70 = f32[384,1,16,64]{0,3,2,1:T(8,128)} fusion(f32[384,1,16,64]{0,3,2,1:T(8,128)S(1)} %transpose.64, f32[384,1,16,64]{0,3,2,1:T(8,128)S(1)} %bitcast.253, f32[16]{0:T(128)S(1)} %copy-done.11, f32[384,16]{0,1:T(8,128)S(1)} %fusion.140, bf16[4,1,16,64,128]{4,3,2,1,0:T(8,128)(2,1)} %all-gather.8.cloned.1.call-done, f32[16]{0:T(128)S(1)} %get-tuple-element.189, ...), kind=kOutput, calls=%fused_computation.77 | convolution fusion | flops 611844096 | bytes 7988108 | tf_op jit(solution)/shard_map/tgn,ghpn->tghp/dot_general | solution.py:149
  332.4 8.8 %fusion.47 = bf16[384,4096]{1,0:T(8,128)(2,1)} fusion(bf16[1,1024,4096]{2,1,0:T(8,128)(2,1)} %param.23, f32[1024]{0:T(1024)S(1)} %bitcast.257, f32[384]{0:T(512)S(1)} %add_rsqrt_fusion, f32[384,1,1024]{2,0,1:T(8,128)S(1)} %copy.121, bf16[387,1,2304]{2,0,1:T(8,128)(2,1)S(1)} %copy-done.1), kind=kOutput, calls=%fused_computation.58 | convolution fusion | flops 3226337280 | bytes 13899776 | tf_op jit(solution)/shard_map/dot_general | solution.py:158
  341.2 40.1 %reduce-scatter.2.cloned.1.call-done = bf16[384,512]{1,0:T(8,128)(2,1)} async-done(((bf16[384,4096]{1,0:T(8,128)(2,1)}), bf16[384,512]{1,0:T(8,128)(2,1)}) %reduce-scatter.2.cloned.1.call-update) | async-done | bytes 393232 | tf_op jit(solution)/shard_map/reduce_scatter | solution.py:163
  (124 shorter events, 41.3 us)
Async XLA Ops:
  6.5 2.8 copy-start.4
  6.5 160.6 %all-gather.6.cloned.1.call-start = ((), (), s32[]{:S(2)}) async-start(), calls=%async_computation.2 | async-start | bytes 20545536 | tf_op jit(solution)/shard_map/all_gather | solution.py:22
  13.1 4.6 %copy-start.9 = (f32[16]{0:T(128)S(1)}, f32[16]{0:T(128)}, u32[]{:S(2)}) copy-start(f32[16]{0:T(128)} %param.18) | copy-start | bytes 196
  13.1 43.0 %all-to-all-start = ((bf16[384,8,512]{2,0,1:T(8,128)(2,1)}), bf16[384,8,512]{2,0,1:T(8,128)(2,1)}, u32[]{:S(2)}, u32[]{:S(2)}) async-start(bf16[384,8,512]{2,0,1:T(8,128)(2,1)} %copy.105), calls=%async_computation | async-start | bytes 6291456 | tf_op jit(solution)/shard_map/all_to_all | solution.py:115
  17.7 280.5 %all-gather.10.cloned.1.call-start = ((), (), s32[]{:S(2)}) async-start(), calls=%async_computation.5 | async-start | bytes 2359296 | tf_op jit(solution)/shard_map/all_gather | solution.py:41
  59.5 0.8 copy-start.6
  62.4 6.0 %copy-start.5 = (f32[4,1,1280]{2,1,0:T(1,128)S(1)}, f32[4,1,1280]{2,1,0:T(1,128)}, u32[]{:S(2)}) copy-start(f32[4,1,1280]{2,1,0:T(1,128)} %param.20) | copy-start | bytes 61444
  62.5 6.1 %copy-start.7 = (f32[1,1280]{1,0:T(1,128)S(1)}, f32[1,1280]{1,0:T(1,128)}, u32[]{:S(2)}) copy-start(f32[1,1280]{1,0:T(1,128)} %param.21) | copy-start | bytes 15364
  64.4 10.2 %collective-permute-start = (bf16[3,4096]{1,0:T(4,128)(2,1)S(1)}, bf16[3,4096]{1,0:T(4,128)(2,1)S(1)}, u32[]{:S(2)}, u32[]{:S(2)}) collective-permute-start(bf16[3,4096]{1,0:T(4,128)(2,1)S(1)} %copy.107), channel_id=1, source_target_pairs={{0,8},{8,16},{16,24},{24,32},{32,40},{40,48},{48,56},{56,64},{64,7... | collective-permute-start | bytes 73736 | tf_op jit(solution)/shard_map/ppermute | solution.py:17
  181.3 1.3 copy-start
  182.7 3.8 copy-start.2
  182.7 0.7 copy-start.10
  193.4 65.7 %copy-start.12 = (u32[256]{0:T(256)S(1)}, u32[256]{0:T(256)}, u32[]{:S(2)}) copy-start(u32[256]{0:T(256)} %constant.77) | copy-start | bytes 3076
  258.8 66.2 %all-gather.8.cloned.1.call-start = ((), (), s32[]{:S(2)}) async-start(), calls=%async_computation.3 | async-start | bytes 1310720 | tf_op jit(solution)/shard_map/all_gather | solution.py:41
  301.0 80.4 %reduce-scatter.2.cloned.1.call-start = ((), (), s32[]{:S(2)}) async-start(), calls=%async_computation.4 | async-start | bytes 3538944 | tf_op jit(solution)/shard_map/reduce_scatter | solution.py:163
  310.5 14.6 %copy-start.3 = (f32[384,1,1024]{0,2,1:T(8,128)S(1)}, f32[384,1,1024]{0,2,1:T(8,128)}, u32[]{:S(2)}) copy-start(f32[384,1,1024]{0,2,1:T(8,128)} %copy.120) | copy-start | bytes 4718596
  310.5 14.6 %copy-start.11 = (f32[16]{0:T(128)S(1)}, f32[16]{0:T(128)}, u32[]{:S(2)}) copy-start(f32[16]{0:T(128)} %param.19) | copy-start | bytes 196
  329.7 2.0 copy-start.1
  329.7 2.7 copy-start.8
Sparse Core Ops, SparseCore 0:
  9.9 157.1 all-gather.5
  258.9 39.2 all-gather.9
  301.1 23.8 all-gather.7
  341.4 39.9 reduce-scatter.1
